TPU v7x, 128 devices: a whole 4x4x4 slice. The times are simulated.
128 devices in a mesh: expert: 4 (over y_hi, core), shard: 32 (over z, y_lo, x).
Axes of the slice: x: 4, y: 4 (y_hi: 2, y_lo: 2; y = y_hi * 2 + y_lo), z: 4, core: 2. Of those that a mesh axis runs over, the one named last changes fastest.
Arguments:
- w_gate: float32 [128, 2048, 768], P('expert', 'shard'), may hold values from -0.25 to 0.25
- w_up: float32 [128, 2048, 768], P('expert', 'shard'), may hold values from -0.25 to 0.25
- router_weight: float32 [2048, 128], P('shard', 'expert'), may hold values from -0.125 to 0.125
- router_gain: float32 [2048], P('shard'), may hold values from 0.25 to 1.75
Outputs:
- serve_gate: bfloat16 [128, 2048, 768], P('expert', None, 'shard')
- serve_up: bfloat16 [128, 2048, 768], P('expert', None, 'shard')
- scale_gate: float32 [128, 768], P('expert', 'shard')
- scale_up: float32 [128, 768], P('expert', 'shard')
- serve_router: bfloat16 [2048, 128], replicated
All inputs are finite; a program needn't handle non-finite values. Where the computation divides by a largest or mean magnitude, that divisor is 1e-20 or more.
Results may differ from a plain program's by a relative error of at most 0.001.
Values may be sent and summed in bfloat16 or wider, within the bound.
A program may use at most 128 MiB of HBM per device.

v0:
```python
import jax
import jax.numpy as jnp
from jax import lax
from jax.sharding import PartitionSpec as P


def from_everyone(value, axis):
    size = lax.axis_size(axis)
    return lax.all_to_all(
        jnp.broadcast_to(value[None], (size, *value.shape)), axis, 0, 0, tiled=True
    )


def taken_together(value, axis):
    everything = from_everyone(value, axis)
    return jnp.max(everything, axis=0)


def packed_total(arrays, axis):
    ends = [0]
    for a in arrays:
        ends.append(ends[-1] + a.size)
    so_far = taken_together(jnp.concatenate([a.ravel() for a in arrays]), axis)
    return tuple((so_far[b:e].reshape(a.shape) for a, b, e in zip(arrays, ends, ends[1:])))


def joined_along(pieces, dim):
    lengths = list(pieces.shape[1:])
    lengths[dim] *= pieces.shape[0]
    return jnp.moveaxis(pieces, 0, dim).reshape(lengths)


def gather_directly(value, axis, dim):
    pieces = from_everyone(value, axis)
    return joined_along(pieces, dim)


def body(w_gate, w_up, router_weight, router_gain):
    scale_gate, scale_up = packed_total(
        (jnp.max(jnp.abs(w_gate), axis=1), jnp.max(jnp.abs(w_up), axis=1)), "shard"
    )
    narrow_gate, narrow_up = (
        (w_gate / jnp.expand_dims(scale_gate, 1)).astype(jnp.bfloat16),
        (w_up / jnp.expand_dims(scale_up, 1)).astype(jnp.bfloat16),
    )
    serve_gate, serve_up = (
        lax.all_to_all(narrow_gate, "shard", split_axis=2, concat_axis=1, tiled=True),
        lax.all_to_all(narrow_up, "shard", split_axis=2, concat_axis=1, tiled=True),
    )
    scale_gate = lax.dynamic_slice_in_dim(
        scale_gate, lax.axis_index("shard") * serve_gate.shape[2], serve_gate.shape[2], axis=1
    )
    scale_up = lax.dynamic_slice_in_dim(
        scale_up, lax.axis_index("shard") * serve_up.shape[2], serve_up.shape[2], axis=1
    )
    part_router = (router_weight * router_gain[:, None]).astype(jnp.bfloat16)
    row_router = gather_directly(part_router, "shard", 0)
    serve_router = gather_directly(row_router, "expert", 1)
    return (serve_gate, serve_up, scale_gate, scale_up, serve_router)


def solution(mesh):
    return jax.shard_map(
        body,
        mesh=mesh,
        in_specs=(
            P("expert", "shard", None),
            P("expert", "shard", None),
            P("shard", "expert"),
            P("shard"),
        ),
        out_specs=(
            P("expert", None, "shard"),
            P("expert", None, "shard"),
            P("expert", "shard"),
            P("expert", "shard"),
            P(),
        ),
        check_vma=False,
    )
```

profile of v0, /device:TPU:0, one launch (start us, length us, event | category | flops | bytes accessed | tf_op | source)
XLA Modules:
  0.0 286.1 jit_solution(14400901637273972531)
XLA Ops:
  0.6 0.7 multiply_convert_fusion
  1.4 0.8 reshape.59
  2.2 9.3 %all-to-all-start.3 = ((bf16[32,2,1024]{2,1,0:T(2,128)(2,1)}), bf16[32,2,1024]{2,1,0:T(2,128)(2,1)S(1)}, u32[]{:S(2)}, u32[]{:S(2)}) async-start(bf16[32,2,1024]{2,1,0:T(2,128)(2,1)} %reshape.59), calls=%async_computation.3 | async-start | bytes 262144 | tf_op jit(solution)/shard_map/all_to_all | solution.py:9
  11.5 3.5 %abs_reduce_fusion.1 = f32[32,768]{1,0:T(8,128)S(1)} fusion(f32[32,64,768]{2,1,0:T(8,128)} %param.4), kind=kLoop, calls=%fused_computation.3 | loop fusion | flops 3121152 | bytes 6389760 | tf_op jit(solution)/shard_map/reduce_max | solution.py:40
  15.1 3.5 %abs_reduce_fusion = f32[32,768]{1,0:T(8,128)S(1)} fusion(f32[32,64,768]{2,1,0:T(8,128)} %param.5), kind=kLoop, calls=%fused_computation.2 | loop fusion | flops 3121152 | bytes 6389760 | tf_op jit(solution)/shard_map/reduce_max | solution.py:40
  18.7 1.6 all-to-all-done.3
  20.3 6.5 %broadcast_in_dim.8 = f32[32,1,49152]{2,1,0:T(1,128)} broadcast(f32[49152]{0:T(1024)S(1)} %pad_maximum_fusion), dimensions={2} | broadcast | bytes 6488064 | tf_op jit(solution)/shard_map/broadcast_in_dim | solution.py:10
  26.8 6.9 %all-to-all-start = ((f32[32,1,49152]{2,1,0:T(1,128)}), f32[32,1,49152]{2,1,0:T(1,128)}, u32[]{:S(2)}, u32[]{:S(2)}) async-start(f32[32,1,49152]{2,1,0:T(1,128)} %broadcast_in_dim.8), calls=%async_computation | async-start | bytes 12582912 | tf_op jit(solution)/shard_map/all_to_all | solution.py:9
  33.7 12.7 %copy.63 = f32[32,64,768]{1,0,2:T(8,128)} copy(f32[32,64,768]{2,1,0:T(8,128)} %param.4) | data formatting | bytes 12582912 | tf_op args[0]
  46.4 0.2 reshape.60
  46.6 0.1 copy.70
  46.7 0.3 broadcast_in_dim.10
  47.0 70.2 %all-to-all-done = f32[32,1,49152]{2,1,0:T(1,128)} async-done(((f32[32,1,49152]{2,1,0:T(1,128)}), f32[32,1,49152]{2,1,0:T(1,128)}, u32[]{:S(2)}, u32[]{:S(2)}) %all-to-all-start) | async-done | bytes 6291488 | tf_op jit(solution)/shard_map/all_to_all | solution.py:9
  117.2 0.8 broadcast_in_dim.11
  118.1 4.2 %all-to-all-start.4 = ((bf16[4,2048,32]{1,2,0:T(8,128)(2,1)}), bf16[4,2048,32]{1,2,0:T(8,128)(2,1)S(1)}, u32[]{:S(2)}, u32[]{:S(2)}) async-start(bf16[4,2048,32]{1,2,0:T(8,128)(2,1)} %broadcast_in_dim.11), calls=%async_computation.4 | async-start | bytes 1048576 | tf_op jit(solution)/shard_map/all_to_all | solution.py:9
  122.2 8.7 %reduce_max.29 = f32[49152]{0:T(1024)S(1)} reduce(f32[32,1,49152]{2,1,0:T(1,128)} %all-to-all-done, f32[]{:T(128)} %constant.5.clone.1), dimensions={0,1}, to_apply=%region_2.0 | reduce | flops 1523712 | bytes 6488068 | tf_op jit(solution)/shard_map/reduce_max | solution.py:16
  130.9 0.0 copy-start.1
  131.0 0.2 copy.62
  131.1 9.9 %fusion.1 = bf16[768,32,64]{2,1,0:T(8,128)(2,1)} fusion(f32[32,64,768]{1,0,2:T(8,128)} %copy.63, f32[32,768]{0,1:T(8,128)S(1)} %copy.62), kind=kLoop, calls=%fused_computation.9 | loop fusion | flops 3145728 | bytes 9535488
  141.0 0.0 copy-done.1
  141.0 8.7 %reshape.55 = bf16[32,2,24576]{2,1,0:T(2,128)(2,1)} reshape(bf16[768,32,64]{2,1,0:T(8,128)(2,1)} %fusion.1) | data formatting | bytes 6291456
  149.7 0.0 all-to-all-done.4
  149.7 0.0 copy-start
  149.7 0.8 copy-done
  150.5 17.1 %all-to-all-start.1 = ((bf16[32,2,24576]{2,1,0:T(2,128)(2,1)}), bf16[32,2,24576]{2,1,0:T(2,128)(2,1)S(1)}, u32[]{:S(2)}, u32[]{:S(2)}) async-start(bf16[32,2,24576]{2,1,0:T(2,128)(2,1)} %reshape.55), calls=%async_computation.1 | async-start | bytes 6291456 | tf_op jit(solution)/shard_map/all_to_all | solution.py:47
  167.6 12.7 %copy.67 = f32[32,64,768]{1,0,2:T(8,128)} copy(f32[32,64,768]{2,1,0:T(8,128)} %param.5) | data formatting | bytes 12582912 | tf_op args[1]
  180.3 0.7 slice.33
  180.9 1.1 copy.66
  182.0 9.9 %fusion.2 = bf16[768,32,64]{2,1,0:T(8,128)(2,1)} fusion(f32[32,64,768]{1,0,2:T(8,128)} %copy.67, f32[32,768]{0,1:T(8,128)S(1)} %copy.66), kind=kLoop, calls=%fused_computation.10 | loop fusion | flops 3145728 | bytes 9535488
  191.8 8.7 %reshape.57 = bf16[32,2,24576]{2,1,0:T(2,128)(2,1)} reshape(bf16[768,32,64]{2,1,0:T(8,128)(2,1)} %fusion.2) | data formatting | bytes 6291456
  200.6 9.8 %all-to-all-done.1 = bf16[32,2,24576]{2,1,0:T(2,128)(2,1)S(1)} async-done(((bf16[32,2,24576]{2,1,0:T(2,128)(2,1)}), bf16[32,2,24576]{2,1,0:T(2,128)(2,1)S(1)}, u32[]{:S(2)}, u32[]{:S(2)}) %all-to-all-start.1) | async-done | bytes 3145760 | tf_op jit(solution)/shard_map/all_to_all | solution.py:47
  210.4 8.1 %all-to-all-start.2 = ((bf16[32,2,24576]{2,1,0:T(2,128)(2,1)}), bf16[32,2,24576]{2,1,0:T(2,128)(2,1)}, u32[]{:S(2)}, u32[]{:S(2)}) async-start(bf16[32,2,24576]{2,1,0:T(2,128)(2,1)} %reshape.57), calls=%async_computation.2 | async-start | bytes 6291456 | tf_op jit(solution)/shard_map/all_to_all | solution.py:48
  218.4 2.0 copy.73
  220.5 0.8 constant_dynamic-slice_fusion
  221.3 0.7 copy.71
  222.0 0.7 copy.72
  222.7 6.2 %reshape.56 = bf16[768,32,64]{2,1,0:T(8,128)(2,1)} reshape(bf16[32,2,24576]{2,1,0:T(2,128)(2,1)S(1)} %all-to-all-done.1) | data formatting | bytes 6291456
  228.8 9.5 %copy.65 = bf16[32,32,64,24]{2,1,3,0:T(8,128)(2,1)} copy(bf16[32,32,64,24]{2,0,3,1:T(8,128)(2,1)} %bitcast.28) | data formatting | bytes 6291456 | tf_op jit(solution)/shard_map/all_to_all | solution.py:47
  238.3 9.7 %all_to_all.40 = bf16[32,2048,24]{1,2,0:T(8,128)(2,1)} reshape(bf16[32,32,64,24]{2,1,3,0:T(8,128)(2,1)} %copy.65) | data formatting | bytes 6291456 | tf_op jit(solution)/shard_map/all_to_all | solution.py:47
  248.0 10.2 %all-to-all-done.2 = bf16[32,2,24576]{2,1,0:T(2,128)(2,1)} async-done(((bf16[32,2,24576]{2,1,0:T(2,128)(2,1)}), bf16[32,2,24576]{2,1,0:T(2,128)(2,1)}, u32[]{:S(2)}, u32[]{:S(2)}) %all-to-all-start.2) | async-done | bytes 3145760 | tf_op jit(solution)/shard_map/all_to_all | solution.py:48
  258.2 8.7 %reshape.58 = bf16[768,32,64]{2,1,0:T(8,128)(2,1)} reshape(bf16[32,2,24576]{2,1,0:T(2,128)(2,1)} %all-to-all-done.2) | data formatting | bytes 6291456
  266.9 9.5 %copy.69 = bf16[32,32,64,24]{2,1,3,0:T(8,128)(2,1)} copy(bf16[32,32,64,24]{2,0,3,1:T(8,128)(2,1)} %bitcast.29) | data formatting | bytes 6291456 | tf_op jit(solution)/shard_map/all_to_all | solution.py:48
  276.4 9.7 %all_to_all.44 = bf16[32,2048,24]{1,2,0:T(8,128)(2,1)} reshape(bf16[32,32,64,24]{2,1,3,0:T(8,128)(2,1)} %copy.69) | data formatting | bytes 6291456 | tf_op jit(solution)/shard_map/all_to_all | solution.py:48
  (6 shorter events, 0.1 us)
Async XLA Ops:
  2.2 18.0 %all-to-all-start.3 = ((bf16[32,2,1024]{2,1,0:T(2,128)(2,1)}), bf16[32,2,1024]{2,1,0:T(2,128)(2,1)S(1)}, u32[]{:S(2)}, u32[]{:S(2)}) async-start(bf16[32,2,1024]{2,1,0:T(2,128)(2,1)} %reshape.59), calls=%async_computation.3 | async-start | bytes 262144 | tf_op jit(solution)/shard_map/all_to_all | solution.py:9
  26.8 90.4 %all-to-all-start = ((f32[32,1,49152]{2,1,0:T(1,128)}), f32[32,1,49152]{2,1,0:T(1,128)}, u32[]{:S(2)}, u32[]{:S(2)}) async-start(f32[32,1,49152]{2,1,0:T(1,128)} %broadcast_in_dim.8), calls=%async_computation | async-start | bytes 12582912 | tf_op jit(solution)/shard_map/all_to_all | solution.py:9
  118.1 31.7 %all-to-all-start.4 = ((bf16[4,2048,32]{1,2,0:T(8,128)(2,1)}), bf16[4,2048,32]{1,2,0:T(8,128)(2,1)S(1)}, u32[]{:S(2)}, u32[]{:S(2)}) async-start(bf16[4,2048,32]{1,2,0:T(8,128)(2,1)} %broadcast_in_dim.11), calls=%async_computation.4 | async-start | bytes 1048576 | tf_op jit(solution)/shard_map/all_to_all | solution.py:9
  130.9 10.0 %copy-start.1 = (f32[32,768]{1,0:T(8,128)}, f32[32,768]{1,0:T(8,128)S(1)}, u32[]{:S(2)}) copy-start(f32[32,768]{1,0:T(8,128)S(1)} %slice.31) | copy-start | bytes 294916
  149.7 0.8 copy-start
  150.5 59.8 %all-to-all-start.1 = ((bf16[32,2,24576]{2,1,0:T(2,128)(2,1)}), bf16[32,2,24576]{2,1,0:T(2,128)(2,1)S(1)}, u32[]{:S(2)}, u32[]{:S(2)}) async-start(bf16[32,2,24576]{2,1,0:T(2,128)(2,1)} %reshape.55), calls=%async_computation.1 | async-start | bytes 6291456 | tf_op jit(solution)/shard_map/all_to_all | solution.py:47
  210.4 47.9 %all-to-all-start.2 = ((bf16[32,2,24576]{2,1,0:T(2,128)(2,1)}), bf16[32,2,24576]{2,1,0:T(2,128)(2,1)}, u32[]{:S(2)}, u32[]{:S(2)}) async-start(bf16[32,2,24576]{2,1,0:T(2,128)(2,1)} %reshape.57), calls=%async_computation.2 | async-start | bytes 6291456 | tf_op jit(solution)/shard_map/all_to_all | solution.py:48
where the time goes:
time: 291 us; the launch traced here: 286 us
  local copies, waits for them, and re-layouts  112 us (38%)
  waiting for transfers between devices  91.8 us (32%)
  starting transfers between devices  45.5 us (16%)
  other arithmetic  36.2 us (12%)
    all_to_all x3, waiting for transfers between devices, from_everyone(): lax.all_to_all(jnp.broadcast_to(value[None], (size, *value.shape)), axis,...  71.8 us
    unnamed x16, local copies, waits for them, and re-layouts  63 us
    all_to_all x3, starting transfers between devices, from_everyone(): lax.all_to_all(jnp.broadcast_to(value[None], (size, *value.shape)), axis,...  20.3 us
    unnamed x2, other arithmetic  19.7 us
    all_to_all x2, local copies, waits for them, and re-layouts, body(): lax.all_to_all(narrow_gate, 'shard', split_axis=2, concat_axis=1, tiled=T...  19.2 us
    all_to_all x2, local copies, waits for them, and re-layouts, body(): lax.all_to_all(narrow_up, 'shard', split_axis=2, concat_axis=1, tiled=True)  19.2 us
    all_to_all x1, starting transfers between devices, body(): lax.all_to_all(narrow_gate, 'shard', split_axis=2, concat_axis=1, tiled=T...  17.1 us
    all_to_all x1, waiting for transfers between devices, body(): lax.all_to_all(narrow_up, 'shard', split_axis=2, concat_axis=1, tiled=True)  10.2 us
  transfers between devices with their start and end apart: 5, of which 4 were waited for; matrix products, arithmetic and copies ran while one was open for 35% of the time, Pallas kernels for 0%

commit v1 on v0

v1 whole, which is shorter than its diff:
```python
import functools

import jax
import jax.numpy as jnp
from jax import lax
from jax.experimental import pallas as pl
from jax.experimental.pallas import tpu as pltpu
from jax.sharding import PartitionSpec as P

MESH = pl.DeviceIdType.MESH
N = 32
CHUNKS = 8
PAIRS = 4
COLS = 24

SLOTS = (
    ((1, 1, 1), (3, 0, 3)),
    ((1, 0, 1), (3, 1, 3)),
    ((1, 1, 3), (3, 0, 1)),
    ((1, 0, 3), (3, 1, 1)),
    ((2, 1, 2),),
    ((2, 0, 2), (0, 1, 0)),
    ((2, 1, 0), (0, 0, 2)),
    ((2, 0, 0), (0, 1, 2)),
    ((2, 1, 1), (0, 0, 3)),
    ((2, 0, 1), (0, 1, 3)),
    ((2, 0, 3), (0, 1, 1)),
    ((2, 1, 3), (0, 0, 1)),
    ((1, 1, 2), (3, 0, 0)),
    ((1, 0, 2), (3, 1, 0)),
    ((3, 0, 2), (1, 1, 0)),
    ((3, 1, 2), (1, 0, 0)),
)
OFFSETS = tuple(o for slot in SLOTS for o in slot)


def partner(me, offset):
    dz, dy, dx = offset
    z, y, x = me // 8, lax.rem(me // 4, 2), lax.rem(me, 4)
    return lax.rem(z + dz, 4) * 8 + lax.rem(y + dy, 2) * 4 + lax.rem(x + dx, 4)


def exchange(
    gate, up, router, gain,
    recv, scale_g, scale_u, rout,
    wbuf, send, lmax, rsbuf, scall, inv, tmp0, tmp1, rtile, rgot, rhalf, rbig,
    load_sem, rs_send, rs_recv, ag_send, ag_recv, r1_send, r1_recv, r2_send, r2_recv, r3_send, r3_recv,
    a_send, a_recv, own_sem, rown_sem,
):
    me = lax.axis_index("shard")
    e = lax.axis_index("expert")
    core = lax.rem(e, 2)

    def load(c):
        src = gate if c < CHUNKS // 2 else up
        row = c % (CHUNKS // 2) * PAIRS
        return pltpu.make_async_copy(
            src.at[pl.ds(row, PAIRS)], wbuf.at[pl.ds(c * PAIRS, PAIRS)], load_sem.at[c]
        )

    for c in range(CHUNKS):
        load(c).start()

    barrier = pltpu.get_barrier_semaphore()
    for o in OFFSETS:
        pl.semaphore_signal(barrier, inc=1, device_id={"shard": partner(me, o)}, device_id_type=MESH)
    for k in range(1, 4):
        pl.semaphore_signal(barrier, inc=1, device_id={"expert": lax.rem(e + k, 4)}, device_id_type=MESH)

    part = router[...] * gain[...]
    for k in range(4):
        rbig[pl.ds(32 * k, 32), pl.ds(0, 64)] = part
    tile = rbig[...].T[:64].astype(jnp.bfloat16)
    rtile[...] = tile
    rgot[e] = tile

    pl.semaphore_wait(barrier, len(OFFSETS) + 3)

    def r1(k):
        return pltpu.make_async_remote_copy(
            src_ref=rtile, dst_ref=rgot.at[e], send_sem=r1_send.at[k - 1], recv_sem=r1_recv.at[k - 1],
            device_id={"expert": lax.rem(e + k, 4)}, device_id_type=MESH,
        )

    for k in range(1, 4):
        r1(k).start()

    for c in range(CHUNKS):
        load(c).wait()

        def pair_max(q, carry, c=c):
            p = c * PAIRS + q
            for h in range(2):
                for j in range(6):
                    block = wbuf[p, pl.ds(64 * h, 64), pl.ds(128 * j, 128)]
                    lmax[p, pl.ds(6 * h + j, 1), :] = jnp.max(jnp.abs(block), axis=0, keepdims=True)

            @pl.when(p != me)
            def _():
                pltpu.make_async_remote_copy(
                    src_ref=lmax.at[p], dst_ref=rsbuf.at[me], send_sem=rs_send, recv_sem=rs_recv,
                    device_id={"shard": p}, device_id_type=MESH,
                ).start()

            return carry

        lax.fori_loop(0, PAIRS, pair_max, 0)

    rsbuf[me] = lmax[me]
    others = pl.ds(0, N - 1)
    pltpu.make_async_copy(rsbuf.at[others], rsbuf.at[others], rs_recv).wait()
    scall[me] = lax.fori_loop(1, N, lambda s, m: jnp.maximum(m, rsbuf[s]), rsbuf[0])
    for o in OFFSETS:
        pltpu.make_async_remote_copy(
            src_ref=scall.at[me], dst_ref=scall.at[me], send_sem=ag_send, recv_sem=ag_recv.at[me],
            device_id={"shard": partner(me, o)}, device_id_type=MESH,
        ).start()

    for k in range(1, 4):
        r1(k).wait_recv()
    lane = lax.broadcasted_iota(jnp.int32, (32, 128), 1) // 32
    rows = pl.ds(pl.multiple_of(core * 32, 32), 32)
    wide = [rgot[k, rows, :].astype(jnp.float32) for k in range(4)]
    merged = jnp.where(lane == 0, wide[0], jnp.where(lane == 1, wide[1], jnp.where(lane == 2, wide[2], wide[3])))
    rhalf[...] = merged.astype(jnp.bfloat16)
    rown = pltpu.make_async_copy(rhalf, rout.at[me, core], rown_sem)
    rown.start()
    for o in OFFSETS:
        pltpu.make_async_remote_copy(
            src_ref=rhalf, dst_ref=rout.at[me, core], send_sem=r2_send, recv_sem=r2_recv,
            device_id={"shard": partner(me, o)}, device_id_type=MESH,
        ).start()

    def chunk(c, carry):
        for q in range(PAIRS):
            p = c * PAIRS + q

            @pl.when(p != me)
            def _():
                pltpu.make_async_copy(scall.at[p], scall.at[p], ag_recv.at[p]).wait()

        def pair(q, carry):
            p = c * PAIRS + q
            inv[...] = 1.0 / scall[p]
            for j in range(6):
                cols = pl.ds(128 * j, 128)
                top = wbuf[p, pl.ds(0, 64), cols] * inv[pl.ds(j, 1), :]
                low = wbuf[p, pl.ds(64, 64), cols] * inv[pl.ds(6 + j, 1), :]
                block = jnp.concatenate([top, low], axis=0)
                send[c, q, cols, :] = block.T.astype(jnp.bfloat16)
            return carry

        lax.fori_loop(0, PAIRS, pair, 0)

        def mine(d):
            return send.at[c, :, pl.ds(pl.multiple_of(d * COLS, 8), COLS), :]

        pltpu.make_async_copy(mine(me), recv.at[c, me], own_sem.at[c]).start()
        for o in OFFSETS:
            d = partner(me, o)
            pltpu.make_async_remote_copy(
                src_ref=mine(d), dst_ref=recv.at[c, me], send_sem=a_send.at[c], recv_sem=a_recv.at[c],
                device_id={"shard": d}, device_id_type=MESH,
            ).start()
        return carry

    lax.fori_loop(0, CHUNKS, chunk, 0)

    first = me * COLS
    j0, off = first // 128, lax.rem(first, 128)
    j1 = jnp.minimum(j0 + 1, 5)

    def pick(r, carry):
        p, h = r // 2, lax.rem(r, 2)
        tmp0[pl.ds(r, 1), :] = scall[p, pl.ds(h * 6 + j0, 1), :]
        tmp1[pl.ds(r, 1), :] = scall[p, pl.ds(h * 6 + j1, 1), :]
        return carry

    lax.fori_loop(0, 64, pick, 0)
    back = lax.rem(128 - off, 128)
    where = lax.broadcasted_iota(jnp.int32, (128, 128), 1) < 128 - off
    own = jnp.where(where, pltpu.roll(tmp0[...], back, 1), pltpu.roll(tmp1[...], back, 1)).T
    scale_g[...] = own[:COLS, 0:32]
    scale_u[...] = own[:COLS, 32:64]

    rown.wait()
    half = rout.at[pl.ds(0, N - 1), 0]
    pltpu.make_async_copy(half, half, r2_recv).wait()
    r3 = pltpu.make_async_remote_copy(
        src_ref=rout.at[:, core], dst_ref=rout.at[:, core], send_sem=r3_send, recv_sem=r3_recv,
        device_id={"expert": e + 1 - 2 * core}, device_id_type=MESH,
    )
    r3.start()

    pltpu.make_async_copy(rsbuf.at[others], rsbuf.at[others], rs_send).wait()
    pltpu.make_async_copy(rsbuf.at[others], rsbuf.at[others], ag_send).wait()
    for k in range(1, 4):
        r1(k).wait_send()
    pltpu.make_async_copy(half, half, r2_send).wait()
    for c in range(CHUNKS):
        pltpu.make_async_copy(recv.at[c, 0], recv.at[c, 0], own_sem.at[c]).wait()
        pltpu.make_async_copy(recv.at[c, others], recv.at[c, others], a_send.at[c]).wait()
        pltpu.make_async_copy(recv.at[c, others], recv.at[c, others], a_recv.at[c]).wait()
    r3.wait()


def merge(recv, sg, su, router, gate, up, og, ou, orouter):
    c = pl.program_id(0)

    def into(out):
        low = lax.broadcasted_iota(jnp.int32, (COLS, 128), 1) < 64
        for q in range(PAIRS):
            for k in range(N // 2):
                a = recv[0, 2 * k, q].astype(jnp.float32)
                b = recv[0, 2 * k + 1, q].astype(jnp.float32)
                lanes = pl.ds(128 * k, 128)
                out[2 * q, :, lanes] = jnp.where(low, a, pltpu.roll(b, 64, 1)).astype(jnp.bfloat16)
                out[2 * q + 1, :, lanes] = jnp.where(low, pltpu.roll(a, 64, 1), b).astype(jnp.bfloat16)

    @pl.when(c < CHUNKS // 2)
    def _():
        into(gate)

    @pl.when(c >= CHUNKS // 2)
    def _():
        into(up)

    orouter[...] = router[...]

    @pl.when(c == 0)
    def _():
        og[...] = sg[...]
        ou[...] = su[...]


def body(w_gate, w_up, router_weight, router_gain):
    f32, bf16 = jnp.float32, jnp.bfloat16
    hbm, vmem = pl.BlockSpec(memory_space=pltpu.HBM), pl.BlockSpec(memory_space=pltpu.VMEM)
    dma = pltpu.SemaphoreType.DMA
    recv, sg, su, rout = pl.pallas_call(
        exchange,
        out_shape=(
            jax.ShapeDtypeStruct((CHUNKS, N, PAIRS, COLS, 128), bf16),
            jax.ShapeDtypeStruct((COLS, 32), f32),
            jax.ShapeDtypeStruct((COLS, 32), f32),
            jax.ShapeDtypeStruct((N, 2, 32, 128), bf16),
        ),
        in_specs=[hbm, hbm, vmem, vmem],
        out_specs=(hbm, vmem, vmem, hbm),
        scratch_shapes=[
            pltpu.VMEM((N, 128, 768), f32),
            pltpu.VMEM((CHUNKS, PAIRS, 768, 128), bf16),
            pltpu.VMEM((N, 12, 128), f32),
            pltpu.VMEM((N, 12, 128), f32),
            pltpu.VMEM((N, 12, 128), f32),
            pltpu.VMEM((12, 128), f32),
            pltpu.VMEM((128, 128), f32),
            pltpu.VMEM((128, 128), f32),
            pltpu.VMEM((64, 128), bf16),
            pltpu.VMEM((4, 64, 128), bf16),
            pltpu.VMEM((32, 128), bf16),
            pltpu.VMEM((128, 128), f32),
            dma((CHUNKS,)), dma, dma, dma, dma((N,)), dma((3,)), dma((3,)), dma, dma, dma, dma,
            dma((CHUNKS,)), dma((CHUNKS,)), dma((CHUNKS,)), dma,
        ],
        compiler_params=pltpu.CompilerParams(
            collective_id=0, has_side_effects=True, vmem_limit_bytes=62 * 2**20
        ),
        name="exchange",
    )(
        w_gate.reshape(16, 128, 768),
        w_up.reshape(16, 128, 768),
        router_weight.T,
        router_gain.reshape(1, 64),
    )
    last = CHUNKS // 2 - 1
    gate, up, sg, su, router = pl.pallas_call(
        merge,
        grid=(CHUNKS,),
        out_shape=(
            jax.ShapeDtypeStruct((32, COLS, 2048), bf16),
            jax.ShapeDtypeStruct((32, COLS, 2048), bf16),
            jax.ShapeDtypeStruct((COLS, 32), f32),
            jax.ShapeDtypeStruct((COLS, 32), f32),
            jax.ShapeDtypeStruct((2048, 128), bf16),
        ),
        in_specs=[
            pl.BlockSpec((1, N, PAIRS, COLS, 128), lambda c: (c, 0, 0, 0, 0)),
            pl.BlockSpec((COLS, 32), lambda c: (0, 0)),
            pl.BlockSpec((COLS, 32), lambda c: (0, 0)),
            pl.BlockSpec((256, 128), lambda c: (c, 0)),
        ],
        out_specs=(
            pl.BlockSpec((8, COLS, 2048), lambda c: (jnp.minimum(c, last), 0, 0)),
            pl.BlockSpec((8, COLS, 2048), lambda c: (jnp.maximum(c - last - 1, 0), 0, 0)),
            pl.BlockSpec((COLS, 32), lambda c: (0, 0)),
            pl.BlockSpec((COLS, 32), lambda c: (0, 0)),
            pl.BlockSpec((256, 128), lambda c: (c, 0)),
        ),
        name="merge",
    )(recv, sg, su, rout.reshape(2048, 128))
    return (gate.swapaxes(1, 2), up.swapaxes(1, 2), sg.T, su.T, router)


def solution(mesh):
    return jax.shard_map(
        body,
        mesh=mesh,
        in_specs=(
            P("expert", "shard", None),
            P("expert", "shard", None),
            P("shard", "expert"),
            P("shard"),
        ),
        out_specs=(
            P("expert", None, "shard"),
            P("expert", None, "shard"),
            P("expert", "shard"),
            P("expert", "shard"),
            P(),
        ),
        check_vma=False,
    )
```

time: 291 us -> 102 us (0.35); the launches traced: 286 us -> 101 us
  local copies, waits for them, and re-layouts: 112 us -> 0 us
  Pallas kernels: 0 us -> 101 us
  waiting for transfers between devices: 91.8 us -> 0 us
  starting transfers between devices: 45.5 us -> 0 us
  other arithmetic: 36.2 us -> 0 us
    pallas_call x0 -> x2, Pallas kernels: none -> 101 us  [the longest x1 91.6 us: body(): pl.pallas_call(exchange, out_shape=(jax.ShapeDtypeStruct((CHUNKS, N, PAIR...]
    all_to_all x5 -> x0, waiting for transfers between devices: 91.8 us -> none  [the longest x3 71.8 us: from_everyone(): lax.all_to_all(jnp.broadcast_to(value[None], (size, *value.shape)), axis,...]
    unnamed x16 -> x0, local copies, waits for them, and re-layouts: 63 us -> none
    all_to_all x5 -> x0, starting transfers between devices: 45.5 us -> none  [the longest x3 20.3 us: from_everyone(): lax.all_to_all(jnp.broadcast_to(value[None], (size, *value.shape)), axis,...]
    all_to_all x5 -> x0, local copies, waits for them, and re-layouts: 38.5 us -> none  [the longest x2 19.2 us: body(): lax.all_to_all(narrow_gate, 'shard', split_axis=2, concat_axis=1, tiled=T...]
    unnamed x2 -> x0, other arithmetic: 19.7 us -> none
    reduce_max x3 -> x0, other arithmetic: 15.8 us -> none  [the longest x1 8.66 us: taken_together(): return jnp.max(everything, axis=0)]
    broadcast_in_dim x3 -> x0, local copies, waits for them, and re-layouts: 7.64 us -> none  [from_everyone(): jnp.broadcast_to(value[None], (size, *value.shape))]
  transfers between devices with their start and end apart: 5 -> 0, of which waited for: 4 -> 0; matrix products, arithmetic and copies ran while one was open for 35% -> 0% of each run, Pallas kernels for 0% -> 0%
where the time goes in v1:
time: 102 us; the launch traced here: 101 us
  Pallas kernels  101 us (99%)
    pallas_call x1, Pallas kernels, body(): pl.pallas_call(exchange, out_shape=(jax.ShapeDtypeStruct((CHUNKS, N, PAIR...  91.6 us
    pallas_call x1, Pallas kernels, body(): pl.pallas_call(merge, grid=(CHUNKS,), out_shape=(jax.ShapeDtypeStruct((32...  9.03 us

profile of v1, /device:TPU:0, one launch (start us, length us, event | category | flops | bytes accessed | tf_op | source)
XLA Modules:
  0.0 101.3 jit_solution(17471336572355607063)
XLA Ops:
  0.6 91.6 %exchange.1 = (bf16[8,32,4,24,128]{4,3,2,1,0:T(8,128)(2,1)}, f32[24,32]{1,0:T(8,128)}, f32[24,32]{1,0:T(8,128)}, bf16[32,2,32,128]{3,2,1,0:T(8,128)(2,1)}) custom-call(f32[16,128,768]{2,1,0:T(8,128)} %bitcast.9, f32[16,128,768]{2,1,0:T(8,128)} %bitcast.10, f32[32,64]{1,0:T(8,128)} %bitcast.12, f32[1,64]{1,0:T(1,128)} %bitcast.13), custom_call_target="tpu_custom_call" | custom-call | tf_op jit(solution)/shard_map/exchange/pallas_call | solution.py:240
  92.3 9.0 %merge.1 = (bf16[32,24,2048]{2,1,0:T(8,128)(2,1)}, bf16[32,24,2048]{2,1,0:T(8,128)(2,1)}, f32[24,32]{1,0:T(8,128)}, f32[24,32]{1,0:T(8,128)}, bf16[2048,128]{1,0:T(8,128)(2,1)}) custom-call(bf16[8,32,4,24,128]{4,3,2,1,0:T(8,128)(2,1)} %get-tuple-element.14.recv, f32[24,32]{1,0:T(8,128)} %get-tuple-element.15.sg, f32[24,32]{1,0:T(8,128)} %get-tuple-element.16.su, ...), custom_call_target="tpu_custom_call" | custom-call | tf_op jit(solution)/shard_map/merge/pallas_call | solution.py:277
